TPU v7x, 32 devices: a whole 2x2x4 slice. The times are simulated.
32 devices in a mesh: sp: 16 (over z, x, core), tp: 2 (over y).
Axes of the slice: x: 2, y: 2, z: 4, core: 2. Of those that a mesh axis runs over, the one named last changes fastest.
Arguments:
- activations: bfloat16 [2, 2048, 8192], P(None, 'sp', 'tp'), may hold values from -250 to 250
- norm_gain: bfloat16 [8192], P('tp'), may hold values from 0.5 to 1.5
- keep_bits: int32 [2, 2048, 1024], P(None, 'sp', 'tp'), may hold values from 0 to 255, as said below
- key_value_weight: bfloat16 [1024, 8192], P('sp', 'tp'), may hold values from -0.0625 to 0.0625
- queries: bfloat16 [2, 2048, 4096], P('tp', 'sp'), may hold values from -68 to 68
- segment: int32 [4096], replicated, may hold values from 0 to 15, never falling along the last dimension, each value on 1 to 512 neighbouring positions
- cotangent: bfloat16 [2, 2048, 4096], P('tp', 'sp'), may hold values from -12 to 12
Outputs:
- attended: bfloat16 [2, 2048, 4096], P('tp', 'sp')
- grad_queries: bfloat16 [2, 2048, 4096], P('tp', 'sp')
- grad_activations: bfloat16 [2, 2048, 8192], P(None, 'sp', 'tp')
- grad_weight: float32 [1024, 8192], P('sp', 'tp')
- grad_gain: float32 [8192], P('tp')
Inputs may be any that keep to these rules, and one draw needn't show every extreme that they name: Bit j of keep_bits[a, b, w] is the keep flag of feature 8 w + j. segment numbers never fall along the sequence; each document covers 1 to 512 positions, and one covers exactly 512.
All inputs are finite; a program needn't handle non-finite values.
Results may differ from a plain program's by a relative error of at most 0.012.
The roundings to bfloat16 on the way count: a program that leaves them out, or rounds other values in their place, can miss the bound.
Values may be sent and summed in bfloat16 or wider, within the bound.
A program may use at most 128 MiB of HBM per device.

v0:
```python
import jax
import jax.numpy as jnp
from jax import lax
from jax.sharding import PartitionSpec as P

D = 8192
HQ = 32
KVH = 4
HD = 128
DOC = 512
GROUP = 8
EPS = 1e-05
KEEP_RATE = 0.9
MASKED_SCORE = -1e30


def shifted(block, axis, distance):
    devices = range(lax.axis_size(axis))
    route = [(i - distance, i) for i in devices if i - distance in devices]
    return lax.ppermute(block, axis, route)


def unpack_flags(words):
    shifts = jnp.arange(8, dtype=jnp.int32)
    flags = jnp.bitwise_and(jnp.right_shift(words[..., None], shifts), 1)
    return flags.reshape(words.shape[:-1] + (words.shape[-1] * 8,)).astype(jnp.float32)


def group_sum(per_head, group_size):
    row_count, head_count, width = per_head.shape
    summed = jnp.sum(
        per_head.reshape(row_count, head_count // group_size, group_size, width), axis=2
    )
    return summed.reshape(row_count, head_count // group_size * width).astype(jnp.bfloat16)


def block_attention(query_block, pair_window, grad_block, allowed):
    score_scale = HD ** (-0.5)
    key_part = pair_window[:, :, :HD]
    value_part = pair_window[:, :, HD:]
    scores = (
        jnp.einsum("qhd,khd->hqk", query_block, key_part, preferred_element_type=jnp.float32)
        * score_scale
    )
    scores = jnp.where(allowed[None], scores, MASKED_SCORE)
    row_max = jnp.max(scores, axis=2, keepdims=True)
    weights = jnp.exp(scores - row_max)
    probabilities = weights / jnp.sum(weights, axis=2, keepdims=True)
    probs_low = probabilities.astype(jnp.bfloat16)
    attended = jnp.einsum(
        "hqk,khd->qhd", probs_low, value_part, preferred_element_type=jnp.float32
    ).astype(jnp.bfloat16)
    grad_probs = jnp.einsum(
        "qhd,khd->hqk", grad_block, value_part, preferred_element_type=jnp.float32
    )
    row_inner = jnp.sum(probabilities * grad_probs, axis=2, keepdims=True)
    grad_scores = (probabilities * (grad_probs - row_inner)).astype(jnp.bfloat16)
    grad_query = (
        jnp.einsum("hqk,khd->qhd", grad_scores, key_part, preferred_element_type=jnp.float32)
        * score_scale
    ).astype(jnp.bfloat16)
    grad_keys = (
        jnp.einsum("hqk,qhd->khd", grad_scores, query_block, preferred_element_type=jnp.float32)
        * score_scale
    )
    grad_values = jnp.einsum(
        "hqk,qhd->khd", probs_low, grad_block, preferred_element_type=jnp.float32
    )
    return (attended, grad_query, jnp.concatenate([grad_keys, grad_values], axis=2))


def run_blocks(query_rows, grad_rows, pair_rows, seg_query, seg_keys):
    block_count = query_rows.shape[0] // DOC
    head_count = query_rows.shape[1]
    causal = (
        jnp.arange(2 * DOC, dtype=jnp.int32)[None, :]
        <= jnp.arange(DOC, dtype=jnp.int32)[:, None] + DOC
    )

    def attend_step(pending, block_index):
        offset = block_index * DOC
        query_block = lax.dynamic_slice_in_dim(query_rows, offset, DOC, 0)
        grad_block = lax.dynamic_slice_in_dim(grad_rows, offset, DOC, 0)
        pair_window = lax.dynamic_slice_in_dim(pair_rows, offset, 2 * DOC, 0)
        block_segs = lax.dynamic_slice_in_dim(seg_query, offset, DOC, 0)
        window_segs = lax.dynamic_slice_in_dim(seg_keys, offset, 2 * DOC, 0)
        allowed = causal & (block_segs[:, None] == window_segs[None, :])
        attended, grad_query, grad_window = block_attention(
            query_block, pair_window, grad_block, allowed
        )
        return (grad_window[DOC:], (attended, grad_query, pending + grad_window[:DOC]))

    return lax.scan(
        attend_step,
        jnp.zeros((DOC, head_count, 2 * HD), jnp.float32),
        jnp.arange(block_count, dtype=jnp.int32),
    )


def on_device(activations, norm_gain, keep_bits, key_value_weight, queries, segment, cotangent):
    sp_size = lax.axis_size("sp")
    tp_size = lax.axis_size("tp")
    tp_index = lax.axis_index("tp")
    block_count, row_count, local_width = activations.shape
    seq_length = row_count * sp_size * tp_size
    query_span = row_count * sp_size
    heads_here = HQ // sp_size
    gain_wide = norm_gain.astype(jnp.float32)
    input_wide = activations.astype(jnp.float32)
    square_total = lax.psum(jnp.sum(input_wide * input_wide, axis=2), "tp")
    inv_rms = lax.rsqrt(square_total[..., None] / D + EPS)
    drop_scale = unpack_flags(keep_bits) / KEEP_RATE
    normed = (input_wide * inv_rms * gain_wide * drop_scale).astype(jnp.bfloat16)
    weight_full = lax.all_gather(key_value_weight, "sp", axis=0, tiled=True)
    pair_tokens = lax.psum_scatter(
        jnp.einsum("arf,cf->arc", normed, weight_full, preferred_element_type=jnp.float32),
        "tp",
        scatter_dimension=0,
        tiled=True,
    )[0].astype(jnp.bfloat16)
    pair_heads = pair_tokens.reshape(row_count, KVH, 2 * HD)
    query_tokens = queries[0].reshape(row_count, HQ, HD)
    grad_tokens = cotangent[0].reshape(row_count, HQ, HD)
    query_here = lax.all_to_all(query_tokens, "sp", split_axis=1, concat_axis=0, tiled=True)
    pair_every = lax.all_gather(pair_heads, "sp", axis=0, tiled=True)
    first_head = lax.axis_index("sp") * heads_here
    owner_head = (first_head + jnp.arange(heads_here, dtype=jnp.int32)) // GROUP
    selector = (owner_head[:, None] == jnp.arange(KVH, dtype=jnp.int32)[None, :]).astype(
        jnp.bfloat16
    )
    pair_here = jnp.einsum(
        "pgc,jg->pjc", pair_every, selector, preferred_element_type=jnp.float32
    ).astype(jnp.bfloat16)
    grad_here = lax.all_to_all(grad_tokens, "sp", split_axis=1, concat_axis=0, tiled=True)
    rim_pairs = shifted(pair_here[query_span - DOC :], "tp", 1)
    pair_extended = jnp.concatenate([rim_pairs, pair_here], axis=0)
    segment_padded = jnp.concatenate([jnp.full((DOC,), -1, jnp.int32), segment])
    segment_keys = lax.dynamic_slice_in_dim(
        segment_padded, tp_index * query_span, query_span + DOC, 0
    )
    segment_query = segment_keys[DOC:]
    final_tail, (outputs, query_grads, finished) = run_blocks(
        query_here, grad_here, pair_extended, segment_query, segment_keys
    )
    rim_back = shifted(finished[0], "tp", -1)
    tail_grad = final_tail + rim_back
    pair_grad_heads = jnp.concatenate(
        [finished[1:].reshape(query_span - DOC, heads_here, 2 * HD), tail_grad], axis=0
    ).astype(jnp.bfloat16)
    attended_heads = outputs.reshape(query_span, heads_here, HD)
    query_grad_heads = query_grads.reshape(query_span, heads_here, HD)
    attended_tokens, query_grad_tokens, pair_grad_tokens = (
        lax.all_to_all(attended_heads, "sp", split_axis=0, concat_axis=1, tiled=True),
        lax.all_to_all(query_grad_heads, "sp", split_axis=0, concat_axis=1, tiled=True),
        lax.all_to_all(pair_grad_heads, "sp", split_axis=0, concat_axis=1, tiled=True),
    )
    pair_grad_rows = group_sum(pair_grad_tokens.astype(jnp.float32), GROUP)
    pair_grad_all = lax.all_gather(pair_grad_rows[None], "tp", axis=0, tiled=True)
    hidden_grad = jnp.einsum(
        "arc,cf->arf", pair_grad_all, weight_full, preferred_element_type=jnp.float32
    )
    grad_weight = lax.psum_scatter(
        jnp.einsum("arc,arf->cf", pair_grad_all, normed, preferred_element_type=jnp.float32),
        "sp",
        scatter_dimension=0,
        tiled=True,
    ) * seq_length ** (-0.5)
    scaled = hidden_grad * drop_scale
    upstream = scaled * gain_wide
    row_dots = lax.psum(jnp.sum(upstream * input_wide, axis=2), "tp")[..., None]
    grad_activations = (
        inv_rms * upstream - input_wide * (inv_rms * inv_rms * inv_rms) * row_dots / D
    ).astype(jnp.bfloat16)
    gain_local = jnp.sum(scaled * input_wide * inv_rms, axis=(0, 1))
    grad_gain = lax.psum(gain_local, "sp") * seq_length ** (-0.5)
    attended = attended_tokens.reshape(1, row_count, HQ * HD)
    grad_queries = query_grad_tokens.reshape(1, row_count, HQ * HD)
    return (attended, grad_queries, grad_activations, grad_weight, grad_gain)


def solution(mesh):
    return jax.shard_map(
        on_device,
        mesh=mesh,
        in_specs=(
            P(None, "sp", "tp"),
            P("tp"),
            P(None, "sp", "tp"),
            P("sp", "tp"),
            P("tp", "sp", None),
            P(),
            P("tp", "sp", None),
        ),
        out_specs=(
            P("tp", "sp", None),
            P("tp", "sp", None),
            P(None, "sp", "tp"),
            P("sp", "tp"),
            P("tp"),
        ),
        check_vma=False,
    )
```

profile of v0, /device:TPU:0, one launch (start us, length us, event | category | flops | bytes accessed | tf_op | source)
XLA Modules:
  0.0 660.8 jit_solution(8027859273964167711)
XLA Ops:
  12.1 5.8 copy.119
  18.6 5.9 psum.21
  25.1 4.7 fusion.44
  29.8 57.4 %all-gather.3.cloned.1.call-done = bf16[1024,4096]{1,0:T(8,128)(2,1)} async-done(((bf16[64,4096]{1,0:T(8,128)(2,1)}), bf16[1024,4096]{1,0:T(8,128)(2,1)}) %all-gather.3.cloned.1.call-update) | async-done | bytes 8388624 | tf_op jit(solution)/shard_map/all_gather | solution.py:114
  87.2 7.4 %fusion.36 = f32[2,128,1024]{2,1,0:T(8,128)} fusion(bf16[2,128,4096]{2,1,0:T(8,128)(2,1)} %fusion.44, bf16[1024,4096]{1,0:T(8,128)(2,1)} %all-gather.3.cloned.1.call-done), kind=kOutput, calls=%fused_computation.53 | convolution fusion | flops 2147483648 | bytes 11534336 | tf_op jit(solution)/shard_map/arf,cf->arc/dot_general | solution.py:116
  94.6 19.1 %reduce-scatter.3.cloned.1.call-done = f32[1,128,1024]{2,1,0:T(8,128)} async-done(((f32[2,128,1024]{2,1,0:T(8,128)}), f32[1,128,1024]{2,1,0:T(8,128)}) %reduce-scatter.3.cloned.1.call-update) | async-done | bytes 524304 | tf_op jit(solution)/shard_map/reduce_scatter | solution.py:115
  117.0 5.6 all-to-all-start.1
  123.9 30.0 %all-to-all-done.1 = bf16[128,32,128]{0,2,1:T(8,128)(2,1)S(1)} async-done(((bf16[128,32,128]{0,2,1:T(8,128)(2,1)}), bf16[128,32,128]{0,2,1:T(8,128)(2,1)S(1)}, u32[]{:S(2)}, u32[]{:S(2)}) %all-to-all-start.1) | async-done | bytes 1048608 | tf_op jit(solution)/shard_map/all_to_all | solution.py:134
  153.9 6.8 %all-to-all-start = ((bf16[128,32,128]{0,2,1:T(8,128)(2,1)}), bf16[128,32,128]{0,2,1:T(8,128)(2,1)S(1)}, u32[]{:S(2)}, u32[]{:S(2)}) async-start(bf16[128,32,128]{0,2,1:T(8,128)(2,1)} %bitcast), calls=%async_computation | async-start | bytes 2097152 | tf_op jit(solution)/shard_map/all_to_all | solution.py:124
  160.8 33.3 %all-gather.5.cloned.1.call-done = bf16[2048,4,256]{2,1,0:T(4,128)(2,1)} async-done(((bf16[128,4,256]{2,1,0:T(4,128)(2,1)}), bf16[2048,4,256]{2,1,0:T(4,128)(2,1)}) %all-gather.5.cloned.1.call-update) | async-done | bytes 4194320 | tf_op jit(solution)/shard_map/all_gather | solution.py:125
  201.2 5.1 collective-permute-start
  208.4 8.4 %collective-permute-done = bf16[512,2,256]{2,1,0:T(2,128)(2,1)} collective-permute-done((bf16[512,2,256]{2,1,0:T(2,128)(2,1)}, bf16[512,2,256]{2,1,0:T(2,128)(2,1)}, u32[]{:S(2)}, u32[]{:S(2)}) %collective-permute-start) | collective-permute-done | bytes 524320 | tf_op jit(solution)/shard_map/ppermute | solution.py:20
  216.9 9.7 %pad_maximum_fusion.1 = bf16[2560,2,256]{2,1,0:T(2,128)(2,1)} fusion(bf16[2048,2,256]{2,1,0:T(2,128)(2,1)} %copy-done.10, bf16[512,2,256]{2,1,0:T(2,128)(2,1)} %collective-permute-done), kind=kLoop, calls=%fused_computation.77 | loop fusion | flops 1310720 | bytes 5242880 | tf_op jit(solution)/shard_map/concatenate | solution.py:136
  227.7 87.9 %while.17 = (s32[]{:T(128)}, f32[512,2,256]{0,2,1:T(8,128)}, bf16[4,512,2,128]{3,1,0,2:T(8,128)(2,1)}, bf16[4,512,2,128]{3,1,0,2:T(8,128)(2,1)}, f32[4,512,2,256...) while((s32[]{:T(128)}, f32[512,2,256]{0,2,1:T(8,128)}, ...), condition=%wide.region_7.8_spmd.clone, body=%wide.region_3.7_spmd.clone.sunk | while | flops 1631453184 | bytes 125355472 | solution.py:93
  315.6 5.3 copy.133
  329.5 20.6 %collective-permute-done.1 = f32[512,2,256]{2,0,1:T(8,128)} collective-permute-done((f32[512,2,256]{2,0,1:T(8,128)}, f32[512,2,256]{2,0,1:T(8,128)}, u32[]{:S(2)}, u32[]{:S(2)}) %collective-permute-start.1) | collective-permute-done | bytes 1048608 | tf_op jit(solution)/shard_map/ppermute | solution.py:20
  351.8 12.8 %copy.135 = bf16[2048,2,256]{2,1,0:T(2,128)(2,1)S(1)} copy(bf16[2048,2,256]{2,0,1:T(8,128)(2,1)S(1)} %pad_maximum_fusion.2) | data formatting | bytes 4194304 | tf_op jit(solution)/shard_map/concatenate | solution.py:147
  364.7 50.7 %all_to_all.75 = bf16[2048,2,256]{2,1,0:T(2,128)(2,1)S(1)} all-to-all(bf16[2048,2,256]{2,1,0:T(2,128)(2,1)S(1)} %copy.135), channel_id=1, replica_groups=mesh['sp'=16,'tp'=2] {'sp'}, dimensions={0} | all-to-all | bytes 4194304 | tf_op jit(solution)/shard_map/all_to_all | solution.py:155
  415.4 12.2 %convert_reduce_fusion = f32[2048,256]{1,0:T(8,128)} fusion(bf16[2048,2,256]{2,1,0:T(2,128)(2,1)S(1)} %all_to_all.75), kind=kLoop, calls=%fused_computation.72 | loop fusion | flops 1572864 | bytes 4194304 | tf_op jit(solution)/shard_map/reduce_sum | solution.py:31
  429.7 9.8 %all_gather.11 = bf16[2,128,1024]{2,1,0:T(8,128)(2,1)S(1)} all-gather(bf16[1,128,1024]{2,1,0:T(8,128)(2,1)S(1)} %copy.137), channel_id=1, replica_groups=mesh['sp'=16,'tp'=2] {'tp'}, dimensions={0}, use_global_device_ids=true | all-gather | bytes 786432 | tf_op jit(solution)/shard_map/all_gather | solution.py:158
  440.4 8.1 %convolution_bitcast_fusion.1 = f32[1024,4096]{1,0:T(8,128)} fusion(bf16[2,128,1024]{2,1,0:T(8,128)(2,1)S(1)} %all_gather.11, bf16[2,128,4096]{2,1,0:T(8,128)(2,1)S(1)} %copy-done.9), kind=kOutput, calls=%fused_computation.50 | convolution fusion | flops 2147483648 | bytes 19398656 | tf_op jit(solution)/shard_map/arc,arf->cf/dot_general | solution.py:163
  449.7 9.4 %copy.125 = bf16[2048,2,128]{2,1,0:T(2,128)(2,1)} copy(bf16[2048,2,128]{2,0,1:T(8,128)(2,1)S(1)} %bitcast.97) | data formatting | bytes 2097152 | tf_op jit(solution)/shard_map/reshape | solution.py:150
  459.2 4.6 all-to-all-start.2
  463.7 9.5 %copy.129 = bf16[2048,2,128]{2,1,0:T(2,128)(2,1)} copy(bf16[2048,2,128]{2,0,1:T(8,128)(2,1)S(1)} %bitcast.98) | data formatting | bytes 2097152 | tf_op jit(solution)/shard_map/reshape | solution.py:151
  473.2 13.4 %all-to-all-done.2 = bf16[2048,2,128]{2,1,0:T(2,128)(2,1)S(1)} async-done(((bf16[2048,2,128]{2,1,0:T(2,128)(2,1)}), bf16[2048,2,128]{2,1,0:T(2,128)(2,1)S(1)}, u32[]{:S(2)}, u32[]{:S(2)}) %all-to-all-start.2) | async-done | bytes 1048608 | tf_op jit(solution)/shard_map/all_to_all | solution.py:153
  486.6 17.4 %all-to-all-start.3 = ((bf16[2048,2,128]{2,1,0:T(2,128)(2,1)}), bf16[2048,2,128]{2,1,0:T(2,128)(2,1)S(1)}, u32[]{:S(2)}, u32[]{:S(2)}) async-start(bf16[2048,2,128]{2,1,0:T(2,128)(2,1)} %copy.129), calls=%async_computation.4 | async-start | bytes 2097152 | tf_op jit(solution)/shard_map/all_to_all | solution.py:154
  508.0 34.9 %all-to-all-done.3 = bf16[2048,2,128]{2,1,0:T(2,128)(2,1)S(1)} async-done(((bf16[2048,2,128]{2,1,0:T(2,128)(2,1)}), bf16[2048,2,128]{2,1,0:T(2,128)(2,1)S(1)}, u32[]{:S(2)}, u32[]{:S(2)}) %all-to-all-start.3) | async-done | bytes 1048608 | tf_op jit(solution)/shard_map/all_to_all | solution.py:154
  547.0 10.3 %fusion.51 = (f32[4096]{0:T(1024)S(1)}, f32[2,128]{1,0:T(2,128)S(1)}, f32[2,128,4096]{2,1,0:T(8,128)}) fusion(bf16[2,128,4096]{2,1,0:T(8,128)(2,1)S(1)} %copy-done.6, f32[2,128]{1,0:T(2,128)S(1)} %copy-done.22, f32[4096]{0:T(1024)S(1)} %copy-done.17, s32[2,128,4096]{2,1,0:T(8,128)} %copy.119, s32[4096]{0:T(1024)S(1)} %copy-done.19, ...), kind=kOutput, calls=%fused_computation.71 | convolution fusion | flops 2160062208 | bytes 19449856 | tf_op jit(solution)/shard_map/arc,cf->arf/dot_general | solution.py:159
  557.3 4.9 psum.22
  562.2 72.5 %psum.23 = f32[4096]{0:T(1024)S(1)} all-reduce(f32[4096]{0:T(1024)S(1)} %get-tuple-element.193), channel_id=1, replica_groups=mesh['sp'=16,'tp'=2] {'sp'}, use_global_device_ids=true, to_apply=%region_14.15 | all-reduce | flops 4096 | bytes 32768 | tf_op jit(solution)/shard_map/psum | solution.py:175
  635.3 4.9 fusion.48
  640.2 11.6 %reduce-scatter.5.cloned.1.call-done = f32[64,4096]{1,0:T(8,128)} async-done(((f32[1024,4096]{1,0:T(8,128)}), f32[64,4096]{1,0:T(8,128)}) %reduce-scatter.5.cloned.1.call-update) | async-done | bytes 1048592 | tf_op jit(solution)/shard_map/reduce_scatter | solution.py:162
  (207 shorter events, 131.2 us)
Async XLA Ops:
  7.2 80.0 %all-gather.3.cloned.1.call-start = ((), (), s32[]{:S(2)}) async-start(), calls=%async_computation.7 | async-start | bytes 8912896 | tf_op jit(solution)/shard_map/all_gather | solution.py:114
  7.9 105.8 %reduce-scatter.3.cloned.1.call-start = ((), (), s32[]{:S(2)}) async-start(), calls=%async_computation.8 | async-start | bytes 1572864 | tf_op jit(solution)/shard_map/reduce_scatter | solution.py:115
  8.6 16.4 %copy-start.16 = (f32[4096]{0:T(1024)}, f32[4096]{0:T(1024)S(1)}, u32[]{:S(2)}) copy-start(f32[4096]{0:T(1024)S(1)} %convert_element_type.69) | copy-start | bytes 49156
  12.1 5.9 copy-start.5
  18.1 11.7 %copy-start.18 = (s32[4096]{0:T(1024)}, s32[4096]{0:T(1024)S(1)}, u32[]{:S(2)}) copy-start(s32[4096]{0:T(1024)S(1)} %shift_right_arithmetic.23) | copy-start | bytes 49156
  25.1 4.7 copy-start.21
  29.8 85.9 %copy-start.12 = (bf16[1,128,4096]{2,1,0:T(8,128)(2,1)S(1)}, bf16[1,128,4096]{2,1,0:T(8,128)(2,1)}, u32[]{:S(2)}) copy-start(bf16[1,128,4096]{2,1,0:T(8,128)(2,1)} %param.15) | copy-start | bytes 3145732
  94.5 28.1 %copy-start.13 = (bf16[1,128,4096]{2,1,0:T(8,128)(2,1)S(1)}, bf16[1,128,4096]{2,1,0:T(8,128)(2,1)}, u32[]{:S(2)}) copy-start(bf16[1,128,4096]{2,1,0:T(8,128)(2,1)} %param.13) | copy-start | bytes 3145732
  94.6 99.5 %all-gather.5.cloned.1.call-start = ((), (), s32[]{:S(2)}) async-start(), calls=%async_computation.9 | async-start | bytes 4456448 | tf_op jit(solution)/shard_map/all_gather | solution.py:125
  117.0 36.9 %all-to-all-start.1 = ((bf16[128,32,128]{0,2,1:T(8,128)(2,1)}), bf16[128,32,128]{0,2,1:T(8,128)(2,1)S(1)}, u32[]{:S(2)}, u32[]{:S(2)}) async-start(bf16[128,32,128]{0,2,1:T(8,128)(2,1)} %bitcast.9), calls=%async_computation.2 | async-start | bytes 2097152 | tf_op jit(solution)/shard_map/all_to_all | solution.py:134
  153.9 53.9 %all-to-all-start = ((bf16[128,32,128]{0,2,1:T(8,128)(2,1)}), bf16[128,32,128]{0,2,1:T(8,128)(2,1)S(1)}, u32[]{:S(2)}, u32[]{:S(2)}) async-start(bf16[128,32,128]{0,2,1:T(8,128)(2,1)} %bitcast), calls=%async_computation | async-start | bytes 2097152 | tf_op jit(solution)/shard_map/all_to_all | solution.py:124
  160.7 491.1 %reduce-scatter.5.cloned.1.call-start = ((), (), s32[]{:S(2)}) async-start(), calls=%async_computation.10 | async-start | bytes 17825792 | tf_op jit(solution)/shard_map/reduce_scatter | solution.py:162
  160.8 45.5 %copy-start.20 = (s32[4096]{0:T(1024)S(1)}, s32[4096]{0:T(1024)}, u32[]{:S(2)}) copy-start(s32[4096]{0:T(1024)} %param.14) | copy-start | bytes 49156
  201.2 15.7 %collective-permute-start = (bf16[512,2,256]{2,1,0:T(2,128)(2,1)}, bf16[512,2,256]{2,1,0:T(2,128)(2,1)}, u32[]{:S(2)}, u32[]{:S(2)}) collective-permute-start(bf16[512,2,256]{2,1,0:T(2,128)(2,1)} %slice.35), channel_id=1, source_target_pairs={{0,1},{2,3},{4,5},{6,7},{8,9},{10,11},{12,13},{14,15},{16,17},{18,... | collective-permute-start | bytes 1572872 | tf_op jit(solution)/shard_map/ppermute | solution.py:20
  227.7 6.7 %copy-start.7 = (bf16[2048,2,128]{2,0,1:T(8,128)(2,1)}, bf16[2048,2,128]{2,0,1:T(8,128)(2,1)S(1)}, u32[]{:S(2)}) copy-start(bf16[2048,2,128]{2,0,1:T(8,128)(2,1)S(1)} %get-tuple-element.361) | copy-start | bytes 3145732 | tf_op jit(solution)/shard_map/while
  237.5 3.5 copy-start.1
  249.6 6.7 %copy-start.7 = (bf16[2048,2,128]{2,0,1:T(8,128)(2,1)}, bf16[2048,2,128]{2,0,1:T(8,128)(2,1)S(1)}, u32[]{:S(2)}) copy-start(bf16[2048,2,128]{2,0,1:T(8,128)(2,1)S(1)} %get-tuple-element.361) | copy-start | bytes 3145732 | tf_op jit(solution)/shard_map/while
  259.5 3.5 copy-start.1
  271.6 6.7 %copy-start.7 = (bf16[2048,2,128]{2,0,1:T(8,128)(2,1)}, bf16[2048,2,128]{2,0,1:T(8,128)(2,1)S(1)}, u32[]{:S(2)}) copy-start(bf16[2048,2,128]{2,0,1:T(8,128)(2,1)S(1)} %get-tuple-element.361) | copy-start | bytes 3145732 | tf_op jit(solution)/shard_map/while
  293.6 6.7 %copy-start.7 = (bf16[2048,2,128]{2,0,1:T(8,128)(2,1)}, bf16[2048,2,128]{2,0,1:T(8,128)(2,1)S(1)}, u32[]{:S(2)}) copy-start(bf16[2048,2,128]{2,0,1:T(8,128)(2,1)S(1)} %get-tuple-element.361) | copy-start | bytes 3145732 | tf_op jit(solution)/shard_map/while
  303.4 3.5 copy-start.1
  320.8 7.2 %copy-start.4 = (f32[512,2,256]{0,2,1:T(8,128)S(1)}, f32[512,2,256]{0,2,1:T(8,128)}, u32[]{:S(2)}) copy-start(f32[512,2,256]{0,2,1:T(8,128)} %get-tuple-element.73) | copy-start | bytes 3145732
  323.3 26.8 %collective-permute-start.1 = (f32[512,2,256]{2,0,1:T(8,128)}, f32[512,2,256]{2,0,1:T(8,128)}, u32[]{:S(2)}, u32[]{:S(2)}) collective-permute-start(f32[512,2,256]{2,0,1:T(8,128)} %slice_bitcast_fusion), channel_id=1, source_target_pairs={{1,0},{3,2},{5,4},{7,6},{9,8},{11,10},{13,12},{15,14},{17,16},{19,... | collective-permute-start | bytes 3145736 | tf_op jit(solution)/shard_map/ppermute | solution.py:20
  415.4 25.0 %copy-start.9 = (bf16[2,128,4096]{2,1,0:T(8,128)(2,1)S(1)}, bf16[2,128,4096]{2,1,0:T(8,128)(2,1)}, u32[]{:S(2)}) copy-start(bf16[2,128,4096]{2,1,0:T(8,128)(2,1)} %fusion.44) | copy-start | bytes 6291460
  448.5 15.2 %copy-start.15 = (bf16[4,512,2,128]{3,1,0,2:T(8,128)(2,1)S(1)}, bf16[4,512,2,128]{3,1,0,2:T(8,128)(2,1)}, u32[]{:S(2)}) copy-start(bf16[4,512,2,128]{3,1,0,2:T(8,128)(2,1)} %get-tuple-element.71) | copy-start | bytes 3145732
  459.2 27.5 %all-to-all-start.2 = ((bf16[2048,2,128]{2,1,0:T(2,128)(2,1)}), bf16[2048,2,128]{2,1,0:T(2,128)(2,1)S(1)}, u32[]{:S(2)}, u32[]{:S(2)}) async-start(bf16[2048,2,128]{2,1,0:T(2,128)(2,1)} %copy.125), calls=%async_computation.3 | async-start | bytes 2097152 | tf_op jit(solution)/shard_map/all_to_all | solution.py:153
  486.6 56.3 %all-to-all-start.3 = ((bf16[2048,2,128]{2,1,0:T(2,128)(2,1)}), bf16[2048,2,128]{2,1,0:T(2,128)(2,1)S(1)}, u32[]{:S(2)}, u32[]{:S(2)}) async-start(bf16[2048,2,128]{2,1,0:T(2,128)(2,1)} %copy.129), calls=%async_computation.4 | async-start | bytes 2097152 | tf_op jit(solution)/shard_map/all_to_all | solution.py:154
  505.5 41.4 %copy-start.6 = (bf16[2,128,4096]{2,1,0:T(8,128)(2,1)S(1)}, bf16[2,128,4096]{2,1,0:T(8,128)(2,1)}, u32[]{:S(2)}) copy-start(bf16[2,128,4096]{2,1,0:T(8,128)(2,1)} %param.9) | copy-start | bytes 6291460
  505.5 41.4 %copy-start.17 = (f32[4096]{0:T(1024)S(1)}, f32[4096]{0:T(1024)}, u32[]{:S(2)}) copy-start(f32[4096]{0:T(1024)} %copy-done.16) | copy-start | bytes 49156
  505.5 41.4 %copy-start.19 = (s32[4096]{0:T(1024)S(1)}, s32[4096]{0:T(1024)}, u32[]{:S(2)}) copy-start(s32[4096]{0:T(1024)} %copy-done.18) | copy-start | bytes 49156
  505.5 41.4 %copy-start.22 = (f32[2,128]{1,0:T(2,128)S(1)}, f32[2,128]{1,0:T(2,128)}, u32[]{:S(2)}) copy-start(f32[2,128]{1,0:T(2,128)} %copy-done.21) | copy-start | bytes 3076
  546.9 88.4 %copy-start.23 = (f32[2,128]{1,0:T(2,128)S(1)}, f32[2,128]{1,0:T(2,128)}, u32[]{:S(2)}) copy-start(f32[2,128]{1,0:T(2,128)} %get-tuple-element.227) | copy-start | bytes 3076
  (20 other events, 42.4 us)
Sparse Core Ops, SparseCore 0:
  10.1 77.0 all-gather.2
  94.7 18.9 reduce-scatter.2
  116.4 77.6 all-gather.4
  448.6 203.0 reduce-scatter.4
where the time goes:
time: 669 us; the launch traced here: 661 us
  waiting for transfers between devices  229 us (34%)
  blocking collectives  144 us (22%)
  local copies, waits for them, and re-layouts  98.3 us (15%)
  matrix products  68 us (10%)
  other arithmetic  62.6 us (9%)
  starting transfers between devices  41.1 us (6%)
  between operations  14.3 us (2%)
    psum x1, blocking collectives, on_device(): grad_gain = lax.psum(gain_local, 'sp') * seq_length ** (-0.5)  72.5 us
    all_gather x1, waiting for transfers between devices, on_device(): weight_full = lax.all_gather(key_value_weight, 'sp', axis=0, tiled=True)  57.4 us
    all_to_all x1, blocking collectives, on_device(): lax.all_to_all(pair_grad_heads, 'sp', split_axis=0, concat_axis=1, tiled=...  50.7 us
    all_to_all x1, waiting for transfers between devices, on_device(): lax.all_to_all(query_grad_heads, 'sp', split_axis=0, concat_axis=1, tiled...  34.9 us
    all_gather x1, waiting for transfers between devices, on_device(): pair_every = lax.all_gather(pair_heads, 'sp', axis=0, tiled=True)  33.3 us
    all_to_all x1, waiting for transfers between devices, on_device(): lax.all_to_all(grad_tokens, 'sp', split_axis=1, concat_axis=0, tiled=True)  30 us
    ppermute x2, waiting for transfers between devices, shifted(): return lax.ppermute(block, axis, route)  29 us
    reduce_scatter x1, waiting for transfers between devices, on_device(): lax.psum_scatter(jnp.einsum('arf,cf->arc', normed, weight_full, preferred...  19.1 us
  transfers between devices with their start and end apart: 10, of which 9 were waited for; matrix products, arithmetic and copies ran while one was open for 11% of the time, Pallas kernels for 0%

commit v1 on v0

--- a/solution.py
+++ b/solution.py
@@ -111,7 +111,12 @@
     inv_rms = lax.rsqrt(square_total[..., None] / D + EPS)
     drop_scale = unpack_flags(keep_bits) / KEEP_RATE
     normed = (input_wide * inv_rms * gain_wide * drop_scale).astype(jnp.bfloat16)
-    weight_full = lax.all_gather(key_value_weight, "sp", axis=0, tiled=True)
+    ring = [key_value_weight]
+    for hop in range(15):
+        ring.append(lax.ppermute(ring[-1], "sp", [(dev, (dev + 1) % 16) for dev in range(16)]))
+    weight_full = jnp.roll(
+        jnp.concatenate(ring[::-1], axis=0), (lax.axis_index("sp") + 1) * ring[0].shape[0], axis=0
+    )
     pair_tokens = lax.psum_scatter(
         jnp.einsum("arf,cf->arc", normed, weight_full, preferred_element_type=jnp.float32),
         "tp",

time: 669 us -> 774 us (1.16)
  waiting for transfers between devices: 229 us -> 324 us
  local copies, waits for them, and re-layouts: 98.3 us -> 114 us
    ppermute x0 -> x15, waiting for transfers between devices: none -> 153 us  [on_device(): lax.ppermute(ring[-1], 'sp', [(dev, (dev + 1) % 16) for dev in range(16)])]
    all_gather x1 -> x0, waiting for transfers between devices: 57.4 us -> none  [on_device(): weight_full = lax.all_gather(key_value_weight, 'sp', axis=0, tiled=True)]
    unnamed x41 -> x120, local copies, waits for them, and re-layouts: 11 us -> 26.3 us
  transfers between devices with their start and end apart: 10 -> 24, of which waited for: 9 -> 22; matrix products, arithmetic and copies ran while one was open for 11% -> 10% of each run, Pallas kernels for 0% -> 0%
where the time goes in v1:
time: 774 us; the launch traced here: 766 us
  waiting for transfers between devices  324 us (42%)
  blocking collectives  143 us (18%)
  local copies, waits for them, and re-layouts  114 us (15%)
  matrix products  64.1 us (8%)
  other arithmetic  61.9 us (8%)
  starting transfers between devices  41.7 us (5%)
  between operations  14.8 us (2%)
    ppermute x15, waiting for transfers between devices, on_device(): lax.ppermute(ring[-1], 'sp', [(dev, (dev + 1) % 16) for dev in range(16)])  153 us
    psum x1, blocking collectives, on_device(): grad_gain = lax.psum(gain_local, 'sp') * seq_length ** (-0.5)  72.4 us
    all_to_all x1, blocking collectives, on_device(): lax.all_to_all(pair_grad_heads, 'sp', split_axis=0, concat_axis=1, tiled=...  50.7 us
    all_to_all x1, waiting for transfers between devices, on_device(): lax.all_to_all(query_grad_heads, 'sp', split_axis=0, concat_axis=1, tiled...  34.9 us
    all_gather x1, waiting for transfers between devices, on_device(): pair_every = lax.all_gather(pair_heads, 'sp', axis=0, tiled=True)  32.9 us
    all_to_all x1, waiting for transfers between devices, on_device(): lax.all_to_all(grad_tokens, 'sp', split_axis=1, concat_axis=0, tiled=True)  30 us
    ppermute x2, waiting for transfers between devices, shifted(): return lax.ppermute(block, axis, route)  29.5 us
    unnamed x120, local copies, waits for them, and re-layouts  26.3 us
  transfers between devices with their start and end apart: 24, of which 22 were waited for; matrix products, arithmetic and copies ran while one was open for 10% of the time, Pallas kernels for 0%

profile of v1, /device:TPU:0, one launch (start us, length us, event | category | flops | bytes accessed | tf_op | source)
XLA Modules:
  0.0 765.7 jit_solution(9001245147967531772)
XLA Ops:
  7.8 12.0 %collective-permute-done = bf16[64,4096]{1,0:T(8,128)(2,1)S(1)} collective-permute-done((bf16[64,4096]{1,0:T(8,128)(2,1)}, bf16[64,4096]{1,0:T(8,128)(2,1)S(1)}, u32[]{:S(2)}, u32[]{:S(2)}) %collective-permute-start) | collective-permute-done | bytes 524320 | tf_op jit(solution)/shard_map/ppermute | solution.py:116
  19.8 11.3 %collective-permute-done.1 = bf16[64,4096]{1,0:T(8,128)(2,1)S(1)} collective-permute-done((bf16[64,4096]{1,0:T(8,128)(2,1)S(1)}, bf16[64,4096]{1,0:T(8,128)(2,1)S(1)}, u32[]{:S(2)}, u32[]{:S(2)}) %collective-permute-start.1) | collective-permute-done | bytes 524320 | tf_op jit(solution)/shard_map/ppermute | solution.py:116
  31.1 11.3 %collective-permute-done.2 = bf16[64,4096]{1,0:T(8,128)(2,1)S(1)} collective-permute-done((bf16[64,4096]{1,0:T(8,128)(2,1)S(1)}, bf16[64,4096]{1,0:T(8,128)(2,1)S(1)}, u32[]{:S(2)}, u32[]{:S(2)}) %collective-permute-start.2) | collective-permute-done | bytes 524320 | tf_op jit(solution)/shard_map/ppermute | solution.py:116
  42.4 11.3 %collective-permute-done.3 = bf16[64,4096]{1,0:T(8,128)(2,1)S(1)} collective-permute-done((bf16[64,4096]{1,0:T(8,128)(2,1)S(1)}, bf16[64,4096]{1,0:T(8,128)(2,1)S(1)}, u32[]{:S(2)}, u32[]{:S(2)}) %collective-permute-start.3) | collective-permute-done | bytes 524320 | tf_op jit(solution)/shard_map/ppermute | solution.py:116
  53.7 11.3 %collective-permute-done.4 = bf16[64,4096]{1,0:T(8,128)(2,1)S(1)} collective-permute-done((bf16[64,4096]{1,0:T(8,128)(2,1)S(1)}, bf16[64,4096]{1,0:T(8,128)(2,1)S(1)}, u32[]{:S(2)}, u32[]{:S(2)}) %collective-permute-start.4) | collective-permute-done | bytes 524320 | tf_op jit(solution)/shard_map/ppermute | solution.py:116
  65.0 11.3 %collective-permute-done.5 = bf16[64,4096]{1,0:T(8,128)(2,1)S(1)} collective-permute-done((bf16[64,4096]{1,0:T(8,128)(2,1)S(1)}, bf16[64,4096]{1,0:T(8,128)(2,1)S(1)}, u32[]{:S(2)}, u32[]{:S(2)}) %collective-permute-start.5) | collective-permute-done | bytes 524320 | tf_op jit(solution)/shard_map/ppermute | solution.py:116
  76.3 11.3 %collective-permute-done.6 = bf16[64,4096]{1,0:T(8,128)(2,1)S(1)} collective-permute-done((bf16[64,4096]{1,0:T(8,128)(2,1)S(1)}, bf16[64,4096]{1,0:T(8,128)(2,1)S(1)}, u32[]{:S(2)}, u32[]{:S(2)}) %collective-permute-start.6) | collective-permute-done | bytes 524320 | tf_op jit(solution)/shard_map/ppermute | solution.py:116
  87.6 11.3 %collective-permute-done.7 = bf16[64,4096]{1,0:T(8,128)(2,1)S(1)} collective-permute-done((bf16[64,4096]{1,0:T(8,128)(2,1)S(1)}, bf16[64,4096]{1,0:T(8,128)(2,1)S(1)}, u32[]{:S(2)}, u32[]{:S(2)}) %collective-permute-start.7) | collective-permute-done | bytes 524320 | tf_op jit(solution)/shard_map/ppermute | solution.py:116
  98.9 11.3 %collective-permute-done.8 = bf16[64,4096]{1,0:T(8,128)(2,1)S(1)} collective-permute-done((bf16[64,4096]{1,0:T(8,128)(2,1)S(1)}, bf16[64,4096]{1,0:T(8,128)(2,1)S(1)}, u32[]{:S(2)}, u32[]{:S(2)}) %collective-permute-start.8) | collective-permute-done | bytes 524320 | tf_op jit(solution)/shard_map/ppermute | solution.py:116
  110.2 11.3 %collective-permute-done.9 = bf16[64,4096]{1,0:T(8,128)(2,1)S(1)} collective-permute-done((bf16[64,4096]{1,0:T(8,128)(2,1)S(1)}, bf16[64,4096]{1,0:T(8,128)(2,1)S(1)}, u32[]{:S(2)}, u32[]{:S(2)}) %collective-permute-start.9) | collective-permute-done | bytes 524320 | tf_op jit(solution)/shard_map/ppermute | solution.py:116
  121.5 11.3 %collective-permute-done.10 = bf16[64,4096]{1,0:T(8,128)(2,1)S(1)} collective-permute-done((bf16[64,4096]{1,0:T(8,128)(2,1)S(1)}, bf16[64,4096]{1,0:T(8,128)(2,1)S(1)}, u32[]{:S(2)}, u32[]{:S(2)}) %collective-permute-start.10) | collective-permute-done | bytes 524320 | tf_op jit(solution)/shard_map/ppermute | solution.py:116
  132.9 11.3 %collective-permute-done.11 = bf16[64,4096]{1,0:T(8,128)(2,1)S(1)} collective-permute-done((bf16[64,4096]{1,0:T(8,128)(2,1)S(1)}, bf16[64,4096]{1,0:T(8,128)(2,1)S(1)}, u32[]{:S(2)}, u32[]{:S(2)}) %collective-permute-start.11) | collective-permute-done | bytes 524320 | tf_op jit(solution)/shard_map/ppermute | solution.py:116
  145.7 10.0 %collective-permute-done.12 = bf16[64,4096]{1,0:T(8,128)(2,1)} collective-permute-done((bf16[64,4096]{1,0:T(8,128)(2,1)S(1)}, bf16[64,4096]{1,0:T(8,128)(2,1)}, u32[]{:S(2)}, u32[]{:S(2)}) %collective-permute-start.12) | collective-permute-done | bytes 524320 | tf_op jit(solution)/shard_map/ppermute | solution.py:116
  200.5 18.2 %reduce-scatter.3.cloned.1.call-done = f32[1,128,1024]{2,1,0:T(8,128)} async-done(((f32[2,128,1024]{2,1,0:T(8,128)}), f32[1,128,1024]{2,1,0:T(8,128)}) %reduce-scatter.3.cloned.1.call-update) | async-done | bytes 524304 | tf_op jit(solution)/shard_map/reduce_scatter | solution.py:120
  229.0 30.0 %all-to-all-done.1 = bf16[128,32,128]{0,2,1:T(8,128)(2,1)S(1)} async-done(((bf16[128,32,128]{0,2,1:T(8,128)(2,1)}), bf16[128,32,128]{0,2,1:T(8,128)(2,1)S(1)}, u32[]{:S(2)}, u32[]{:S(2)}) %all-to-all-start.1) | async-done | bytes 1048608 | tf_op jit(solution)/shard_map/all_to_all | solution.py:139
  266.3 32.9 %all-gather.2.cloned.1.call-done = bf16[2048,4,256]{2,1,0:T(4,128)(2,1)} async-done(((bf16[128,4,256]{2,1,0:T(4,128)(2,1)}), bf16[2048,4,256]{2,1,0:T(4,128)(2,1)}) %all-gather.2.cloned.1.call-update) | async-done | bytes 4194320 | tf_op jit(solution)/shard_map/all_gather | solution.py:130
  313.0 8.9 %collective-permute-done.15 = bf16[512,2,256]{2,1,0:T(2,128)(2,1)} collective-permute-done((bf16[512,2,256]{2,1,0:T(2,128)(2,1)}, bf16[512,2,256]{2,1,0:T(2,128)(2,1)}, u32[]{:S(2)}, u32[]{:S(2)}) %collective-permute-start.15) | collective-permute-done | bytes 524320 | tf_op jit(solution)/shard_map/ppermute | solution.py:20
  322.0 9.7 %pad_maximum_fusion.1 = bf16[2560,2,256]{2,1,0:T(2,128)(2,1)} fusion(bf16[2048,2,256]{2,1,0:T(2,128)(2,1)} %copy-done.11, bf16[512,2,256]{2,1,0:T(2,128)(2,1)} %collective-permute-done.15), kind=kLoop, calls=%fused_computation.79 | loop fusion | flops 1310720 | bytes 5242880 | tf_op jit(solution)/shard_map/concatenate | solution.py:141
  332.8 87.8 %while.17 = (s32[]{:T(128)}, f32[512,2,256]{0,2,1:T(8,128)}, bf16[4,512,2,128]{3,1,0,2:T(8,128)(2,1)}, bf16[4,512,2,128]{3,1,0,2:T(8,128)(2,1)}, f32[4,512,2,256...) while((s32[]{:T(128)}, f32[512,2,256]{0,2,1:T(8,128)}, ...), condition=%wide.region_7.8_spmd.clone, body=%wide.region_3.7_spmd.clone.sunk | while | flops 1631453184 | bytes 125355472 | solution.py:93
  434.4 20.6 %collective-permute-done.16 = f32[512,2,256]{2,0,1:T(8,128)} collective-permute-done((f32[512,2,256]{2,0,1:T(8,128)}, f32[512,2,256]{2,0,1:T(8,128)}, u32[]{:S(2)}, u32[]{:S(2)}) %collective-permute-start.16) | collective-permute-done | bytes 1048608 | tf_op jit(solution)/shard_map/ppermute | solution.py:20
  456.8 12.8 %copy.135 = bf16[2048,2,256]{2,1,0:T(2,128)(2,1)S(1)} copy(bf16[2048,2,256]{2,0,1:T(8,128)(2,1)S(1)} %pad_maximum_fusion.2) | data formatting | bytes 4194304 | tf_op jit(solution)/shard_map/concatenate | solution.py:152
  469.6 50.7 %all_to_all.75 = bf16[2048,2,256]{2,1,0:T(2,128)(2,1)S(1)} all-to-all(bf16[2048,2,256]{2,1,0:T(2,128)(2,1)S(1)} %copy.135), channel_id=1, replica_groups=mesh['sp'=16,'tp'=2] {'sp'}, dimensions={0} | all-to-all | bytes 4194304 | tf_op jit(solution)/shard_map/all_to_all | solution.py:160
  520.3 12.2 %convert_reduce_fusion = f32[2048,256]{1,0:T(8,128)} fusion(bf16[2048,2,256]{2,1,0:T(2,128)(2,1)S(1)} %all_to_all.75), kind=kLoop, calls=%fused_computation.74 | loop fusion | flops 1572864 | bytes 4194304 | tf_op jit(solution)/shard_map/reduce_sum | solution.py:31
  534.7 9.8 %all_gather.7 = bf16[2,128,1024]{2,1,0:T(8,128)(2,1)S(1)} all-gather(bf16[1,128,1024]{2,1,0:T(8,128)(2,1)S(1)} %copy.137), channel_id=1, replica_groups=mesh['sp'=16,'tp'=2] {'tp'}, dimensions={0}, use_global_device_ids=true | all-gather | bytes 786432 | tf_op jit(solution)/shard_map/all_gather | solution.py:163
  554.7 9.4 %copy.125 = bf16[2048,2,128]{2,1,0:T(2,128)(2,1)} copy(bf16[2048,2,128]{2,0,1:T(8,128)(2,1)S(1)} %bitcast.97) | data formatting | bytes 2097152 | tf_op jit(solution)/shard_map/reshape | solution.py:155
  568.7 9.5 %copy.129 = bf16[2048,2,128]{2,1,0:T(2,128)(2,1)} copy(bf16[2048,2,128]{2,0,1:T(8,128)(2,1)S(1)} %bitcast.98) | data formatting | bytes 2097152 | tf_op jit(solution)/shard_map/reshape | solution.py:156
  578.2 13.4 %all-to-all-done.2 = bf16[2048,2,128]{2,1,0:T(2,128)(2,1)S(1)} async-done(((bf16[2048,2,128]{2,1,0:T(2,128)(2,1)}), bf16[2048,2,128]{2,1,0:T(2,128)(2,1)S(1)}, u32[]{:S(2)}, u32[]{:S(2)}) %all-to-all-start.2) | async-done | bytes 1048608 | tf_op jit(solution)/shard_map/all_to_all | solution.py:158
  591.6 17.4 %all-to-all-start.3 = ((bf16[2048,2,128]{2,1,0:T(2,128)(2,1)}), bf16[2048,2,128]{2,1,0:T(2,128)(2,1)S(1)}, u32[]{:S(2)}, u32[]{:S(2)}) async-start(bf16[2048,2,128]{2,1,0:T(2,128)(2,1)} %copy.129), calls=%async_computation.4 | async-start | bytes 2097152 | tf_op jit(solution)/shard_map/all_to_all | solution.py:159
  612.9 34.9 %all-to-all-done.3 = bf16[2048,2,128]{2,1,0:T(2,128)(2,1)S(1)} async-done(((bf16[2048,2,128]{2,1,0:T(2,128)(2,1)}), bf16[2048,2,128]{2,1,0:T(2,128)(2,1)S(1)}, u32[]{:S(2)}, u32[]{:S(2)}) %all-to-all-start.3) | async-done | bytes 1048608 | tf_op jit(solution)/shard_map/all_to_all | solution.py:159
  651.9 10.4 %fusion.53 = (f32[4096]{0:T(1024)S(1)}, f32[2,128]{1,0:T(2,128)S(1)}, f32[2,128,4096]{2,1,0:T(8,128)}) fusion(bf16[2,128,4096]{2,1,0:T(8,128)(2,1)S(1)} %copy-done.6, f32[2,128]{1,0:T(2,128)S(1)} %copy-done.45, f32[4096]{0:T(1024)S(1)} %copy-done.39, s32[2,128,4096]{2,1,0:T(8,128)} %copy.119, s32[4096]{0:T(1024)S(1)} %copy-done.41, ...), kind=kOutput, calls=%fused_computation.73 | convolution fusion | flops 2160062208 | bytes 19449860 | tf_op jit(solution)/shard_map/arc,cf->arf/dot_general | solution.py:164
  667.2 72.4 %psum.23 = f32[4096]{0:T(1024)S(1)} all-reduce(f32[4096]{0:T(1024)S(1)} %get-tuple-element.193), channel_id=1, replica_groups=mesh['sp'=16,'tp'=2] {'sp'}, use_global_device_ids=true, to_apply=%region_14.15 | all-reduce | flops 4096 | bytes 32768 | tf_op jit(solution)/shard_map/psum | solution.py:180
  745.2 11.5 %reduce-scatter.5.cloned.1.call-done = f32[64,4096]{1,0:T(8,128)} async-done(((f32[1024,4096]{1,0:T(8,128)}), f32[64,4096]{1,0:T(8,128)}) %reduce-scatter.5.cloned.1.call-update) | async-done | bytes 1048592 | tf_op jit(solution)/shard_map/reduce_scatter | solution.py:167
  (314 shorter events, 216.5 us)
Async XLA Ops:
  7.2 150.8 %copy-start.46 = (bf16[4096]{0:T(1024)(128)(2,1)S(1)}, bf16[4096]{0:T(1024)(128)(2,1)}, u32[]{:S(2)}) copy-start(bf16[4096]{0:T(1024)(128)(2,1)} %param.10) | copy-start | bytes 24580
  7.2 211.6 %reduce-scatter.3.cloned.1.call-start = ((), (), s32[]{:S(2)}) async-start(), calls=%async_computation.7 | async-start | bytes 1572864 | tf_op jit(solution)/shard_map/reduce_scatter | solution.py:120
  7.2 12.6 %collective-permute-start = (bf16[64,4096]{1,0:T(8,128)(2,1)}, bf16[64,4096]{1,0:T(8,128)(2,1)S(1)}, u32[]{:S(2)}, u32[]{:S(2)}) collective-permute-start(bf16[64,4096]{1,0:T(8,128)(2,1)} %param.12), channel_id=1, source_target_pairs={{0,2},{2,4},{4,6},{6,8},{8,10},{10,12},{12,14},{14,16},{16,18},{18... | collective-permute-start | bytes 1572872 | tf_op jit(solution)/shard_map/ppermute | solution.py:116
  19.8 11.3 %collective-permute-start.1 = (bf16[64,4096]{1,0:T(8,128)(2,1)S(1)}, bf16[64,4096]{1,0:T(8,128)(2,1)S(1)}, u32[]{:S(2)}, u32[]{:S(2)}) collective-permute-start(bf16[64,4096]{1,0:T(8,128)(2,1)S(1)} %collective-permute-done), channel_id=1, source_target_pairs={{0,2},{2,4},{4,6},{6,8},{8,10},{10,12},{12,14},{14,16},{16,18},{18... | collective-permute-start | bytes 1572872 | tf_op jit(solution)/shard_map/ppermute | solution.py:116
  31.1 11.3 %collective-permute-start.2 = (bf16[64,4096]{1,0:T(8,128)(2,1)S(1)}, bf16[64,4096]{1,0:T(8,128)(2,1)S(1)}, u32[]{:S(2)}, u32[]{:S(2)}) collective-permute-start(bf16[64,4096]{1,0:T(8,128)(2,1)S(1)} %collective-permute-done.1), channel_id=1, source_target_pairs={{0,2},{2,4},{4,6},{6,8},{8,10},{10,12},{12,14},{14,16},{16,18},{18... | collective-permute-start | bytes 1572872 | tf_op jit(solution)/shard_map/ppermute | solution.py:116
  42.4 101.8 %copy-start.14 = (bf16[64,4096]{1,0:T(8,128)(2,1)}, bf16[64,4096]{1,0:T(8,128)(2,1)S(1)}, u32[]{:S(2)}) copy-start(bf16[64,4096]{1,0:T(8,128)(2,1)S(1)} %collective-permute-done.2) | copy-start | bytes 1572868
  42.4 11.3 %collective-permute-start.3 = (bf16[64,4096]{1,0:T(8,128)(2,1)S(1)}, bf16[64,4096]{1,0:T(8,128)(2,1)S(1)}, u32[]{:S(2)}, u32[]{:S(2)}) collective-permute-start(bf16[64,4096]{1,0:T(8,128)(2,1)S(1)} %collective-permute-done.2), channel_id=1, source_target_pairs={{0,2},{2,4},{4,6},{6,8},{8,10},{10,12},{12,14},{14,16},{16,18},{18... | collective-permute-start | bytes 1572872 | tf_op jit(solution)/shard_map/ppermute | solution.py:116
  53.7 90.5 %copy-start.16 = (bf16[64,4096]{1,0:T(8,128)(2,1)}, bf16[64,4096]{1,0:T(8,128)(2,1)S(1)}, u32[]{:S(2)}) copy-start(bf16[64,4096]{1,0:T(8,128)(2,1)S(1)} %collective-permute-done.3) | copy-start | bytes 1572868
  53.7 11.3 %collective-permute-start.4 = (bf16[64,4096]{1,0:T(8,128)(2,1)S(1)}, bf16[64,4096]{1,0:T(8,128)(2,1)S(1)}, u32[]{:S(2)}, u32[]{:S(2)}) collective-permute-start(bf16[64,4096]{1,0:T(8,128)(2,1)S(1)} %collective-permute-done.3), channel_id=1, source_target_pairs={{0,2},{2,4},{4,6},{6,8},{8,10},{10,12},{12,14},{14,16},{16,18},{18... | collective-permute-start | bytes 1572872 | tf_op jit(solution)/shard_map/ppermute | solution.py:116
  65.0 79.1 %copy-start.18 = (bf16[64,4096]{1,0:T(8,128)(2,1)}, bf16[64,4096]{1,0:T(8,128)(2,1)S(1)}, u32[]{:S(2)}) copy-start(bf16[64,4096]{1,0:T(8,128)(2,1)S(1)} %collective-permute-done.4) | copy-start | bytes 1572868
  65.0 11.3 %collective-permute-start.5 = (bf16[64,4096]{1,0:T(8,128)(2,1)S(1)}, bf16[64,4096]{1,0:T(8,128)(2,1)S(1)}, u32[]{:S(2)}, u32[]{:S(2)}) collective-permute-start(bf16[64,4096]{1,0:T(8,128)(2,1)S(1)} %collective-permute-done.4), channel_id=1, source_target_pairs={{0,2},{2,4},{4,6},{6,8},{8,10},{10,12},{12,14},{14,16},{16,18},{18... | collective-permute-start | bytes 1572872 | tf_op jit(solution)/shard_map/ppermute | solution.py:116
  76.3 67.8 %copy-start.20 = (bf16[64,4096]{1,0:T(8,128)(2,1)}, bf16[64,4096]{1,0:T(8,128)(2,1)S(1)}, u32[]{:S(2)}) copy-start(bf16[64,4096]{1,0:T(8,128)(2,1)S(1)} %collective-permute-done.5) | copy-start | bytes 1572868
  76.3 11.3 %collective-permute-start.6 = (bf16[64,4096]{1,0:T(8,128)(2,1)S(1)}, bf16[64,4096]{1,0:T(8,128)(2,1)S(1)}, u32[]{:S(2)}, u32[]{:S(2)}) collective-permute-start(bf16[64,4096]{1,0:T(8,128)(2,1)S(1)} %collective-permute-done.5), channel_id=1, source_target_pairs={{0,2},{2,4},{4,6},{6,8},{8,10},{10,12},{12,14},{14,16},{16,18},{18... | collective-permute-start | bytes 1572872 | tf_op jit(solution)/shard_map/ppermute | solution.py:116
  87.6 56.6 %copy-start.22 = (bf16[64,4096]{1,0:T(8,128)(2,1)}, bf16[64,4096]{1,0:T(8,128)(2,1)S(1)}, u32[]{:S(2)}) copy-start(bf16[64,4096]{1,0:T(8,128)(2,1)S(1)} %collective-permute-done.6) | copy-start | bytes 1572868
  87.6 11.3 %collective-permute-start.7 = (bf16[64,4096]{1,0:T(8,128)(2,1)S(1)}, bf16[64,4096]{1,0:T(8,128)(2,1)S(1)}, u32[]{:S(2)}, u32[]{:S(2)}) collective-permute-start(bf16[64,4096]{1,0:T(8,128)(2,1)S(1)} %collective-permute-done.6), channel_id=1, source_target_pairs={{0,2},{2,4},{4,6},{6,8},{8,10},{10,12},{12,14},{14,16},{16,18},{18... | collective-permute-start | bytes 1572872 | tf_op jit(solution)/shard_map/ppermute | solution.py:116
  98.9 45.3 %copy-start.24 = (bf16[64,4096]{1,0:T(8,128)(2,1)}, bf16[64,4096]{1,0:T(8,128)(2,1)S(1)}, u32[]{:S(2)}) copy-start(bf16[64,4096]{1,0:T(8,128)(2,1)S(1)} %collective-permute-done.7) | copy-start | bytes 1572868
  98.9 11.3 %collective-permute-start.8 = (bf16[64,4096]{1,0:T(8,128)(2,1)S(1)}, bf16[64,4096]{1,0:T(8,128)(2,1)S(1)}, u32[]{:S(2)}, u32[]{:S(2)}) collective-permute-start(bf16[64,4096]{1,0:T(8,128)(2,1)S(1)} %collective-permute-done.7), channel_id=1, source_target_pairs={{0,2},{2,4},{4,6},{6,8},{8,10},{10,12},{12,14},{14,16},{16,18},{18... | collective-permute-start | bytes 1572872 | tf_op jit(solution)/shard_map/ppermute | solution.py:116
  110.2 11.3 %collective-permute-start.9 = (bf16[64,4096]{1,0:T(8,128)(2,1)S(1)}, bf16[64,4096]{1,0:T(8,128)(2,1)S(1)}, u32[]{:S(2)}, u32[]{:S(2)}) collective-permute-start(bf16[64,4096]{1,0:T(8,128)(2,1)S(1)} %collective-permute-done.8), channel_id=1, source_target_pairs={{0,2},{2,4},{4,6},{6,8},{8,10},{10,12},{12,14},{14,16},{16,18},{18... | collective-permute-start | bytes 1572872 | tf_op jit(solution)/shard_map/ppermute | solution.py:116
  121.5 11.3 %collective-permute-start.10 = (bf16[64,4096]{1,0:T(8,128)(2,1)S(1)}, bf16[64,4096]{1,0:T(8,128)(2,1)S(1)}, u32[]{:S(2)}, u32[]{:S(2)}) collective-permute-start(bf16[64,4096]{1,0:T(8,128)(2,1)S(1)} %collective-permute-done.9), channel_id=1, source_target_pairs={{0,2},{2,4},{4,6},{6,8},{8,10},{10,12},{12,14},{14,16},{16,18},{18... | collective-permute-start | bytes 1572872 | tf_op jit(solution)/shard_map/ppermute | solution.py:116
  132.9 11.3 %collective-permute-start.11 = (bf16[64,4096]{1,0:T(8,128)(2,1)S(1)}, bf16[64,4096]{1,0:T(8,128)(2,1)S(1)}, u32[]{:S(2)}, u32[]{:S(2)}) collective-permute-start(bf16[64,4096]{1,0:T(8,128)(2,1)S(1)} %collective-permute-done.10), channel_id=1, source_target_pairs={{0,2},{2,4},{4,6},{6,8},{8,10},{10,12},{12,14},{14,16},{16,18},{18... | collective-permute-start | bytes 1572872 | tf_op jit(solution)/shard_map/ppermute | solution.py:116
  144.2 11.5 %collective-permute-start.12 = (bf16[64,4096]{1,0:T(8,128)(2,1)S(1)}, bf16[64,4096]{1,0:T(8,128)(2,1)}, u32[]{:S(2)}, u32[]{:S(2)}) collective-permute-start(bf16[64,4096]{1,0:T(8,128)(2,1)S(1)} %collective-permute-done.11), channel_id=1, source_target_pairs={{0,2},{2,4},{4,6},{6,8},{8,10},{10,12},{12,14},{14,16},{16,18},{18... | collective-permute-start | bytes 1572872 | tf_op jit(solution)/shard_map/ppermute | solution.py:116
  155.7 14.2 %collective-permute-start.13 = (bf16[64,4096]{1,0:T(8,128)(2,1)}, bf16[64,4096]{1,0:T(8,128)(2,1)}, u32[]{:S(2)}, u32[]{:S(2)}) collective-permute-start(bf16[64,4096]{1,0:T(8,128)(2,1)} %collective-permute-done.12), channel_id=1, source_target_pairs={{0,2},{2,4},{4,6},{6,8},{8,10},{10,12},{12,14},{14,16},{16,18},{18... | collective-permute-start | bytes 1572872 | tf_op jit(solution)/shard_map/ppermute | solution.py:116
  169.9 11.6 %collective-permute-start.14 = (bf16[64,4096]{1,0:T(8,128)(2,1)}, bf16[64,4096]{1,0:T(8,128)(2,1)}, u32[]{:S(2)}, u32[]{:S(2)}) collective-permute-start(bf16[64,4096]{1,0:T(8,128)(2,1)} %collective-permute-done.13), channel_id=1, source_target_pairs={{0,2},{2,4},{4,6},{6,8},{8,10},{10,12},{12,14},{14,16},{16,18},{18... | collective-permute-start | bytes 1572872 | tf_op jit(solution)/shard_map/ppermute | solution.py:116
  200.4 98.7 %all-gather.2.cloned.1.call-start = ((), (), s32[]{:S(2)}) async-start(), calls=%async_computation.8 | async-start | bytes 4456448 | tf_op jit(solution)/shard_map/all_gather | solution.py:130
  222.0 36.9 %all-to-all-start.1 = ((bf16[128,32,128]{0,2,1:T(8,128)(2,1)}), bf16[128,32,128]{0,2,1:T(8,128)(2,1)S(1)}, u32[]{:S(2)}, u32[]{:S(2)}) async-start(bf16[128,32,128]{0,2,1:T(8,128)(2,1)} %bitcast.9), calls=%async_computation.2 | async-start | bytes 2097152 | tf_op jit(solution)/shard_map/all_to_all | solution.py:139
  258.9 53.4 %all-to-all-start = ((bf16[128,32,128]{0,2,1:T(8,128)(2,1)}), bf16[128,32,128]{0,2,1:T(8,128)(2,1)S(1)}, u32[]{:S(2)}, u32[]{:S(2)}) async-start(bf16[128,32,128]{0,2,1:T(8,128)(2,1)} %bitcast), calls=%async_computation | async-start | bytes 2097152 | tf_op jit(solution)/shard_map/all_to_all | solution.py:129
  265.7 490.9 %reduce-scatter.5.cloned.1.call-start = ((), (), s32[]{:S(2)}) async-start(), calls=%async_computation.9 | async-start | bytes 17825792 | tf_op jit(solution)/shard_map/reduce_scatter | solution.py:167
  306.3 15.7 %collective-permute-start.15 = (bf16[512,2,256]{2,1,0:T(2,128)(2,1)}, bf16[512,2,256]{2,1,0:T(2,128)(2,1)}, u32[]{:S(2)}, u32[]{:S(2)}) collective-permute-start(bf16[512,2,256]{2,1,0:T(2,128)(2,1)} %slice.35), channel_id=1, source_target_pairs={{0,1},{2,3},{4,5},{6,7},{8,9},{10,11},{12,13},{14,15},{16,17},{18,... | collective-permute-start | bytes 1572872 | tf_op jit(solution)/shard_map/ppermute | solution.py:20
  428.2 26.8 %collective-permute-start.16 = (f32[512,2,256]{2,0,1:T(8,128)}, f32[512,2,256]{2,0,1:T(8,128)}, u32[]{:S(2)}, u32[]{:S(2)}) collective-permute-start(f32[512,2,256]{2,0,1:T(8,128)} %slice_bitcast_fusion), channel_id=1, source_target_pairs={{1,0},{3,2},{5,4},{7,6},{9,8},{11,10},{13,12},{15,14},{17,16},{19,... | collective-permute-start | bytes 3145736 | tf_op jit(solution)/shard_map/ppermute | solution.py:20
  564.1 27.5 %all-to-all-start.2 = ((bf16[2048,2,128]{2,1,0:T(2,128)(2,1)}), bf16[2048,2,128]{2,1,0:T(2,128)(2,1)S(1)}, u32[]{:S(2)}, u32[]{:S(2)}) async-start(bf16[2048,2,128]{2,1,0:T(2,128)(2,1)} %copy.125), calls=%async_computation.3 | async-start | bytes 2097152 | tf_op jit(solution)/shard_map/all_to_all | solution.py:158
  591.6 56.3 %all-to-all-start.3 = ((bf16[2048,2,128]{2,1,0:T(2,128)(2,1)}), bf16[2048,2,128]{2,1,0:T(2,128)(2,1)S(1)}, u32[]{:S(2)}, u32[]{:S(2)}) async-start(bf16[2048,2,128]{2,1,0:T(2,128)(2,1)} %copy.129), calls=%async_computation.4 | async-start | bytes 2097152 | tf_op jit(solution)/shard_map/all_to_all | solution.py:159
  651.9 88.4 %copy-start.47 = (f32[2,128]{1,0:T(2,128)S(1)}, f32[2,128]{1,0:T(2,128)}, u32[]{:S(2)}) copy-start(f32[2,128]{1,0:T(2,128)} %get-tuple-element.227) | copy-start | bytes 3076
  (58 other events, 587.4 us)
Sparse Core Ops, SparseCore 0:
  200.6 18.1 reduce-scatter.2
  221.5 77.6 all-gather.1
  553.6 203.0 reduce-scatter.4
